TPU v7x, 32 devices: a whole 2x2x4 slice. The times are simulated.
32 devices in a mesh: seq: 8 (over z, y), shard: 4 (over x, core).
Axes of the slice: x: 2, y: 2, z: 4, core: 2. Of those that a mesh axis runs over, the one named last changes fastest.
Arguments:
- tokens: bfloat16 [8, 4096, 768], P('shard', 'seq'), may hold values from -6 to 6
- segments: int32 [8, 4096], P('shard'), may hold values from 0 to 20, as said below
- positions: int32 [8, 4096], P('shard', 'seq'), may hold values from 0 to 1999, as said below
- cotangent: bfloat16 [8, 4096, 768], P('shard', 'seq'), may hold values from -6 to 6
- w_qkv: bfloat16 [768, 2304], P('shard'), may hold values from -0.21875 to 0.21875
- w_out: bfloat16 [768, 768], P('shard'), may hold values from -3 to 3
- w_gate: bfloat16 [768, 3072], P('shard'), may hold values from -0.21875 to 0.21875
- w_up: bfloat16 [768, 3072], P('shard'), may hold values from -0.21875 to 0.21875
- w_down: bfloat16 [3072, 768], P('shard'), may hold values from -0.109375 to 0.109375
- ln1_gain: bfloat16 [768], P('shard'), may hold values from 0.099609375 to 1.8984375
- ln1_bias: bfloat16 [768], P('shard'), may hold values from -3 to 3
- ln2_gain: bfloat16 [768], P('shard'), may hold values from 0.099609375 to 1.8984375
- ln2_bias: bfloat16 [768], P('shard'), may hold values from -3 to 3
Outputs:
- output: bfloat16 [8, 4096, 768], P('shard', 'seq')
- input_grad: bfloat16 [8, 4096, 768], P('shard', 'seq')
- grad_w_qkv: float32 [768, 2304], P('shard')
- grad_w_out: float32 [768, 768], P('shard')
- grad_w_gate: float32 [768, 3072], P('shard')
- grad_w_up: float32 [768, 3072], P('shard')
- grad_w_down: float32 [3072, 768], P('shard')
- grad_ln1_gain: float32 [768], P('shard')
- grad_ln1_bias: float32 [768], P('shard')
- grad_ln2_gain: float32 [768], P('shard')
- grad_ln2_bias: float32 [768], P('shard')
Inputs may be any that keep to these rules, and one draw needn't show every extreme that they name: segments[s, t] numbers the documents of sequence s in order from 0 and never falls along t; every document has 200 to 2000 tokens, except that the end of the sequence may cut the last one short. positions[s, t] counts the earlier tokens of the same document of sequence s.
All inputs are finite; a program needn't handle non-finite values.
Results may differ from a plain program's by a relative error of at most 0.025.
Values may be sent and summed in bfloat16 or wider, within the bound.
A program may use at most 256 MiB of HBM per device.

v0:
```python
import math
import jax
import jax.numpy as jnp
from jax import lax
from jax.sharding import PartitionSpec as P

HEADS = 12
HD = 64
EPS = 1e-05
ROPE_BASE = 1000.0


def rope_tables(pos_block):
    half_dim = HD // 2
    freqs = jnp.exp(jnp.arange(half_dim, dtype=jnp.float32) * (-math.log(ROPE_BASE) / half_dim))
    angle = pos_block.astype(jnp.float32)[..., None] * freqs
    return (jnp.cos(angle)[:, :, None, :], jnp.sin(angle)[:, :, None, :])


def rotate(heads, cos_b, sin_b):
    half_dim = heads.shape[-1] // 2
    first = heads[..., :half_dim]
    second = heads[..., half_dim:]
    return jnp.concatenate(
        [first * cos_b - second * sin_b, second * cos_b + first * sin_b], axis=-1
    )


def rotate_back(grads, cos_b, sin_b):
    half_dim = grads.shape[-1] // 2
    first = grads[..., :half_dim]
    second = grads[..., half_dim:]
    return jnp.concatenate(
        [first * cos_b + second * sin_b, second * cos_b - first * sin_b], axis=-1
    )


def norm_fwd(values, gain, bias):
    mean_val = jnp.mean(values, axis=-1, keepdims=True)
    centered = values - mean_val
    variance = jnp.mean(centered * centered, axis=-1, keepdims=True)
    inverse = lax.rsqrt(variance + EPS)
    normed = centered * inverse
    return (normed * gain + bias, normed, inverse)


def norm_back(grad_in, normed, inverse, gain):
    scaled = grad_in * gain
    return inverse * (
        scaled
        - jnp.mean(scaled, axis=-1, keepdims=True)
        - normed * jnp.mean(scaled * normed, axis=-1, keepdims=True)
    )


def head_split(block_rows, seq_count, row_count):
    return block_rows.reshape(seq_count, row_count, HEADS, HD)


def attend(q_heads, q_seg, k_full, v_full, seg_all, block, score_scale):
    seq_count, row_count = (q_heads.shape[0], q_heads.shape[1])
    block_count = k_full.shape[1] // block

    def attend_step(carry, index):
        row_total, value_sum = carry
        start = index * block
        k_part = head_split(lax.dynamic_slice_in_dim(k_full, start, block, 1), seq_count, block)
        v_part = head_split(lax.dynamic_slice_in_dim(v_full, start, block, 1), seq_count, block)
        seg_part = lax.dynamic_slice_in_dim(seg_all, start, block, 1)
        raw = (
            jnp.einsum("sqhd,skhd->shqk", q_heads, k_part, preferred_element_type=jnp.float32)
            * score_scale
        )
        same_doc = q_seg[:, None, :, None] == seg_part[:, None, None, :]
        expo = jnp.where(same_doc, jnp.exp(raw), 0.0)
        row_total = row_total + jnp.sum(expo, axis=-1)
        value_sum = value_sum + jnp.einsum(
            "shqk,skhd->sqhd", expo.astype(jnp.bfloat16), v_part, preferred_element_type=jnp.float32
        )
        return ((row_total, value_sum), None)

    start_carry = (
        jnp.zeros((seq_count, HEADS, row_count), jnp.float32),
        jnp.zeros((seq_count, row_count, HEADS, HD), jnp.float32),
    )
    final, unused = lax.scan(attend_step, start_carry, jnp.arange(block_count, dtype=jnp.int32))
    return final


def back_keys(q_heads, g_heads, delta, q_seg, k_full, v_full, seg_all, block, score_scale):
    seq_count, row_count = (q_heads.shape[0], q_heads.shape[1])
    full_len = k_full.shape[1]
    block_count = full_len // block

    def back_step(carry, index):
        start = index * block
        k_part = head_split(lax.dynamic_slice_in_dim(k_full, start, block, 1), seq_count, block)
        v_part = head_split(lax.dynamic_slice_in_dim(v_full, start, block, 1), seq_count, block)
        seg_part = lax.dynamic_slice_in_dim(seg_all, start, block, 1)
        raw = (
            jnp.einsum("sqhd,skhd->shqk", q_heads, k_part, preferred_element_type=jnp.float32)
            * score_scale
        )
        same_doc = q_seg[:, None, :, None] == seg_part[:, None, None, :]
        expo = jnp.where(same_doc, jnp.exp(raw), 0.0)
        prob_grad = jnp.einsum(
            "sqhd,skhd->shqk", g_heads, v_part, preferred_element_type=jnp.float32
        )
        d_score = (expo * (prob_grad - delta[..., None])).astype(jnp.bfloat16)
        q_grad = carry[0] + jnp.einsum(
            "shqk,skhd->sqhd", d_score, k_part, preferred_element_type=jnp.float32
        )
        k_grad = (
            jnp.einsum("shqk,sqhd->skhd", d_score, q_heads, preferred_element_type=jnp.float32)
            * score_scale
        )
        v_grad = jnp.einsum(
            "shqk,sqhd->skhd",
            expo.astype(jnp.bfloat16),
            g_heads,
            preferred_element_type=jnp.float32,
        )
        k_store = lax.dynamic_update_slice_in_dim(
            carry[1], k_grad.reshape(seq_count, block, HEADS * HD), start, 1
        )
        v_store = lax.dynamic_update_slice_in_dim(
            carry[2], v_grad.reshape(seq_count, block, HEADS * HD), start, 1
        )
        return ((q_grad, k_store, v_store), None)

    q_zero = jnp.zeros((seq_count, row_count, HEADS, HD), jnp.float32)
    kv_zero = jnp.zeros((seq_count, full_len, HEADS * HD), jnp.float32)
    start_carry = (q_zero, kv_zero, kv_zero)
    final, unused = lax.scan(back_step, start_carry, jnp.arange(block_count, dtype=jnp.int32))
    return (final[0] * score_scale,) + tuple(final[1:])


def local(
    tokens,
    segments,
    positions,
    cotangent,
    w_qkv,
    w_out,
    w_gate,
    w_up,
    w_down,
    ln1_gain,
    ln1_bias,
    ln2_gain,
    ln2_bias,
):
    seq_count, row_count, model_width = tokens.shape
    score_scale = HD ** (-0.5)
    q_seg = lax.dynamic_slice_in_dim(segments, lax.axis_index("seq") * row_count, row_count, 1)
    gathered = (
        lax.all_gather(w_qkv, "shard", axis=0, tiled=True),
        lax.all_gather(w_out, "shard", axis=0, tiled=True),
        lax.all_gather(w_gate, "shard", axis=0, tiled=True),
        lax.all_gather(w_up, "shard", axis=0, tiled=True),
        lax.all_gather(w_down, "shard", axis=0, tiled=True),
        lax.all_gather(ln1_gain, "shard", axis=0, tiled=True),
        lax.all_gather(ln1_bias, "shard", axis=0, tiled=True),
        lax.all_gather(ln2_gain, "shard", axis=0, tiled=True),
        lax.all_gather(ln2_bias, "shard", axis=0, tiled=True),
    )
    full_qkv, full_out, full_gate, full_up, full_down, gain_one, bias_one, gain_two, bias_two = (
        gathered
    )
    cos_b, sin_b = rope_tables(positions)
    qkv_all = jnp.einsum("scd,de->sce", tokens, full_qkv, preferred_element_type=jnp.float32)
    q_heads = rotate(
        head_split(qkv_all[..., :model_width], seq_count, row_count), cos_b, sin_b
    ).astype(jnp.bfloat16)
    k_heads = rotate(
        head_split(qkv_all[..., model_width : 2 * model_width], seq_count, row_count), cos_b, sin_b
    ).astype(jnp.bfloat16)
    v_heads = head_split(qkv_all[..., 2 * model_width :], seq_count, row_count).astype(jnp.bfloat16)
    k_local = k_heads.reshape(seq_count, row_count, model_width)
    v_local = v_heads.reshape(seq_count, row_count, model_width)
    k_full, v_full = (
        lax.all_gather(k_local, "seq", axis=1, tiled=True),
        lax.all_gather(v_local, "seq", axis=1, tiled=True),
    )
    row_total, value_sum = attend(q_heads, q_seg, k_full, v_full, segments, row_count, score_scale)
    denom = jnp.transpose(row_total, (0, 2, 1))[..., None]
    attn_out = value_sum / denom
    joined = attn_out.reshape(seq_count, row_count, model_width).astype(jnp.bfloat16)
    tokens_f = tokens.astype(jnp.float32)
    h_one = tokens_f + jnp.einsum(
        "sci,io->sco", joined, full_out, preferred_element_type=jnp.float32
    )
    x_one, normed_one, inverse_one = norm_fwd(
        h_one, gain_one.astype(jnp.float32), bias_one.astype(jnp.float32)
    )
    x_low = x_one.astype(jnp.bfloat16)
    gate_pre = jnp.einsum("scd,df->scf", x_low, full_gate, preferred_element_type=jnp.float32)
    up_pre = jnp.einsum("scd,df->scf", x_low, full_up, preferred_element_type=jnp.float32)
    sigma = jax.nn.sigmoid(gate_pre)
    smooth = gate_pre * sigma
    hidden = (smooth * up_pre).astype(jnp.bfloat16)
    h_two = x_one + jnp.einsum("scf,fd->scd", hidden, full_down, preferred_element_type=jnp.float32)
    result, normed_two, inverse_two = norm_fwd(
        h_two, gain_two.astype(jnp.float32), bias_two.astype(jnp.float32)
    )
    output = result.astype(jnp.bfloat16)
    regathered = (
        lax.all_gather(w_qkv, "shard", axis=0, tiled=True),
        lax.all_gather(w_out, "shard", axis=0, tiled=True),
        lax.all_gather(w_gate, "shard", axis=0, tiled=True),
        lax.all_gather(w_up, "shard", axis=0, tiled=True),
        lax.all_gather(w_down, "shard", axis=0, tiled=True),
        lax.all_gather(ln1_gain, "shard", axis=0, tiled=True),
        lax.all_gather(ln2_gain, "shard", axis=0, tiled=True),
    )
    back_qkv, back_out, back_gate, back_up, back_down, back_gain_one, back_gain_two = regathered
    back_k, back_v = (
        lax.all_gather(k_local, "seq", axis=1, tiled=True),
        lax.all_gather(v_local, "seq", axis=1, tiled=True),
    )
    cot_f = cotangent.astype(jnp.float32)
    grad_gain_two = jnp.sum(cot_f * normed_two, axis=(0, 1))
    grad_bias_two = jnp.sum(cot_f, axis=(0, 1))
    dh_two = norm_back(cot_f, normed_two, inverse_two, back_gain_two.astype(jnp.float32))
    dm_low = dh_two.astype(jnp.bfloat16)
    grad_down = jnp.einsum("scf,scd->fd", hidden, dm_low, preferred_element_type=jnp.float32)
    d_hidden = jnp.einsum("scd,fd->scf", dm_low, back_down, preferred_element_type=jnp.float32)
    d_up = (d_hidden * smooth).astype(jnp.bfloat16)
    d_gate = (d_hidden * up_pre * sigma * (1.0 + gate_pre * (1.0 - sigma))).astype(jnp.bfloat16)
    grad_gate = jnp.einsum("scd,scf->df", x_low, d_gate, preferred_element_type=jnp.float32)
    grad_up = jnp.einsum("scd,scf->df", x_low, d_up, preferred_element_type=jnp.float32)
    dx_one = (
        dh_two
        + jnp.einsum("scf,df->scd", d_gate, back_gate, preferred_element_type=jnp.float32)
        + jnp.einsum("scf,df->scd", d_up, back_up, preferred_element_type=jnp.float32)
    )
    grad_gain_one = jnp.sum(dx_one * normed_one, axis=(0, 1))
    grad_bias_one = jnp.sum(dx_one, axis=(0, 1))
    dh_one = norm_back(dx_one, normed_one, inverse_one, back_gain_one.astype(jnp.float32))
    d_attn = dh_one.astype(jnp.bfloat16)
    grad_out = jnp.einsum("sci,sco->io", joined, d_attn, preferred_element_type=jnp.float32)
    d_joined = jnp.einsum(
        "sco,io->sci", d_attn, back_out, preferred_element_type=jnp.float32
    ).astype(jnp.bfloat16)
    d_heads = head_split(d_joined, seq_count, row_count).astype(jnp.float32)
    g_heads = (d_heads / denom).astype(jnp.bfloat16)
    delta = jnp.transpose(jnp.sum(d_heads * attn_out, axis=-1) / denom[..., 0], (0, 2, 1))
    q_grad, k_all, v_all = back_keys(
        q_heads, g_heads, delta, q_seg, back_k, back_v, segments, row_count, score_scale
    )
    k_sum, v_sum = (
        lax.psum_scatter(k_all.astype(jnp.bfloat16), "seq", scatter_dimension=1, tiled=True).astype(
            jnp.float32
        ),
        lax.psum_scatter(v_all.astype(jnp.bfloat16), "seq", scatter_dimension=1, tiled=True).astype(
            jnp.float32
        ),
    )
    k_grad = head_split(k_sum, seq_count, row_count)
    v_grad = head_split(v_sum, seq_count, row_count)
    q_back = rotate_back(q_grad, cos_b, sin_b).reshape(seq_count, row_count, model_width)
    k_back = rotate_back(k_grad, cos_b, sin_b).reshape(seq_count, row_count, model_width)
    d_qkv = jnp.concatenate(
        [q_back, k_back, v_grad.reshape(seq_count, row_count, model_width)], axis=-1
    ).astype(jnp.bfloat16)
    grad_qkv = jnp.einsum("scd,sce->de", tokens, d_qkv, preferred_element_type=jnp.float32)
    d_tokens = dh_one + jnp.einsum(
        "sce,de->scd", d_qkv, back_qkv, preferred_element_type=jnp.float32
    )
    input_grad = d_tokens.astype(jnp.bfloat16)
    owned = (
        lax.psum_scatter(
            grad_qkv.astype(jnp.bfloat16), "shard", scatter_dimension=0, tiled=True
        ).astype(jnp.float32),
        lax.psum_scatter(
            grad_out.astype(jnp.bfloat16), "shard", scatter_dimension=0, tiled=True
        ).astype(jnp.float32),
        lax.psum_scatter(
            grad_gate.astype(jnp.bfloat16), "shard", scatter_dimension=0, tiled=True
        ).astype(jnp.float32),
        lax.psum_scatter(
            grad_up.astype(jnp.bfloat16), "shard", scatter_dimension=0, tiled=True
        ).astype(jnp.float32),
        lax.psum_scatter(
            grad_down.astype(jnp.bfloat16), "shard", scatter_dimension=0, tiled=True
        ).astype(jnp.float32),
        lax.psum_scatter(
            grad_gain_one.astype(jnp.bfloat16), "shard", scatter_dimension=0, tiled=True
        ).astype(jnp.float32),
        lax.psum_scatter(
            grad_bias_one.astype(jnp.bfloat16), "shard", scatter_dimension=0, tiled=True
        ).astype(jnp.float32),
        lax.psum_scatter(
            grad_gain_two.astype(jnp.bfloat16), "shard", scatter_dimension=0, tiled=True
        ).astype(jnp.float32),
        lax.psum_scatter(
            grad_bias_two.astype(jnp.bfloat16), "shard", scatter_dimension=0, tiled=True
        ).astype(jnp.float32),
    )
    summed = (
        lax.psum(owned[0].astype(jnp.bfloat16), "seq").astype(jnp.float32),
        lax.psum(owned[1].astype(jnp.bfloat16), "seq").astype(jnp.float32),
        lax.psum(owned[2].astype(jnp.bfloat16), "seq").astype(jnp.float32),
        lax.psum(owned[3].astype(jnp.bfloat16), "seq").astype(jnp.float32),
        lax.psum(owned[4].astype(jnp.bfloat16), "seq").astype(jnp.float32),
        lax.psum(owned[5].astype(jnp.bfloat16), "seq").astype(jnp.float32),
        lax.psum(owned[6].astype(jnp.bfloat16), "seq").astype(jnp.float32),
        lax.psum(owned[7].astype(jnp.bfloat16), "seq").astype(jnp.float32),
        lax.psum(owned[8].astype(jnp.bfloat16), "seq").astype(jnp.float32),
    )
    return (
        output,
        input_grad,
        summed[0],
        summed[1],
        summed[2],
        summed[3],
        summed[4],
        summed[5],
        summed[6],
        summed[7],
        summed[8],
    )


def solution(mesh):
    in_specs = (
        P("shard", "seq", None),
        P("shard", None),
        P("shard", "seq"),
        P("shard", "seq", None),
        P("shard", None),
        P("shard", None),
        P("shard", None),
        P("shard", None),
        P("shard", None),
        P("shard"),
        P("shard"),
        P("shard"),
        P("shard"),
    )
    out_specs = (
        P("shard", "seq", None),
        P("shard", "seq", None),
        P("shard", None),
        P("shard", None),
        P("shard", None),
        P("shard", None),
        P("shard", None),
        P("shard"),
        P("shard"),
        P("shard"),
        P("shard"),
    )
    return jax.shard_map(local, mesh=mesh, in_specs=in_specs, out_specs=out_specs, check_vma=False)
```

profile of v0, /device:TPU:0, one launch (start us, length us, event | category | flops | bytes accessed | tf_op | source)
XLA Modules:
  0.0 2137.3 jit_solution(6114114731520905912)
XLA Ops:
  8.0 35.1 %all-gather.8.cloned.1.call-done = bf16[768,2304]{1,0:T(8,128)(2,1)} async-done(((bf16[192,2304]{1,0:T(8,128)(2,1)}), bf16[768,2304]{1,0:T(8,128)(2,1)}) %all-gather.8.cloned.1.call-update) | async-done | bytes 3538960 | tf_op jit(solution)/shard_map/all_gather | solution.py:157
  86.1 144.4 %all-gather.12.cloned.1.call-done = bf16[2,4096,768]{2,1,0:T(8,128)(2,1)} async-done(((bf16[2,512,768]{2,1,0:T(8,128)(2,1)}), bf16[2,4096,768]{2,1,0:T(8,128)(2,1)}) %all-gather.12.cloned.1.call-update) | async-done | bytes 12582928 | tf_op jit(solution)/shard_map/all_gather | solution.py:183
  230.5 16.2 copy.69
  246.7 160.8 %all-gather.10.cloned.1.call-done = bf16[2,4096,768]{1,2,0:T(8,128)(2,1)} async-done(((bf16[2,512,768]{1,2,0:T(8,128)(2,1)}), bf16[2,4096,768]{1,2,0:T(8,128)(2,1)}) %all-gather.10.cloned.1.call-update) | async-done | bytes 12582928 | tf_op jit(solution)/shard_map/all_gather | solution.py:182
  407.5 236.3 %while.28 = (s32[]{:T(128)}, f32[2,12,512]{2,1,0:T(8,128)S(1)}, f32[2,512,12,64]{1,3,2,0:T(8,128)}, s32[2,512]{1,0:T(2,128)S(1)}, s32[8]{0:T(128)S(1)}, /*index=...) while((s32[]{:T(128)}, f32[2,12,512]{2,1,0:T(8,128)S(1)}, ...), condition=%wide.region_2.3_spmd.clone, body=%wide.region_0.2_spmd.clone.sunk | while | flops 1650470912 | bytes 71516400 | solution.py:86
  412.1 11.4 fusion.117
  423.5 12.5 bitcast_add_fusion.4
  440.7 11.4 fusion.117
  452.2 13.5 bitcast_add_fusion.4
  470.3 11.6 fusion.117
  481.9 13.5 bitcast_add_fusion.4
  500.1 11.9 fusion.117
  512.0 14.1 bitcast_add_fusion.4
  530.8 11.5 fusion.117
  542.3 13.4 bitcast_add_fusion.4
  560.3 11.4 fusion.117
  571.7 13.4 bitcast_add_fusion.4
  589.6 11.4 fusion.117
  601.0 13.4 bitcast_add_fusion.4
  619.0 11.4 fusion.117
  630.4 13.4 bitcast_add_fusion.4
  652.9 10.8 fusion.31
  663.7 13.7 multiply_convert_fusion.2
  677.3 9.2 fusion.65
  693.0 18.8 multiply_convert_fusion.1
  711.8 10.1 fusion.25
  722.0 10.4 multiply_reduce_fusion
  757.3 534.2 %while.29 = (s32[]{:T(128)}, f32[2,512,12,64]{1,3,2,0:T(8,128)}, bf16[2,4096,768]{1,2,0:T(8,128)(2,1)}, bf16[2,4096,768]{2,1,0:T(8,128)(2,1)}, s32[8]{0:T(128)S(...) while((s32[]{:T(128)}, f32[2,512,12,64]{1,3,2,0:T(8,128)}, ...), condition=%wide.region_13.14_spmd.clone, body=%wide.region_12.13_spmd.clone.sunk | while | flops 4080533504 | bytes 159449392 | solution.py:134
  762.2 10.1 fusion.128
  774.2 15.9 fusion.129
  809.0 11.7 fusion.130
  828.1 10.1 fusion.128
  840.1 15.9 fusion.129
  875.8 11.7 fusion.130
  895.0 10.1 fusion.128
  906.9 15.9 fusion.129
  942.6 11.7 fusion.130
  961.8 10.1 fusion.128
  973.7 15.9 fusion.129
  1009.4 11.7 fusion.130
  1028.7 10.1 fusion.128
  1040.7 15.9 fusion.129
  1076.3 11.7 fusion.130
  1095.5 10.1 fusion.128
  1107.4 15.9 fusion.129
  1143.1 11.7 fusion.130
  1162.3 10.1 fusion.128
  1174.3 15.9 fusion.129
  1209.9 11.7 fusion.130
  1229.2 10.1 fusion.128
  1241.1 15.9 fusion.129
  1276.8 11.7 fusion.130
  1295.6 203.2 %reduce-scatter.10.cloned.1.call-done = bf16[2,512,768]{1,2,0:T(8,128)(2,1)} async-done(((bf16[2,4096,768]{1,2,0:T(8,128)(2,1)}), bf16[2,512,768]{1,2,0:T(8,128)(2,1)}) %reduce-scatter.10.cloned.1.call-update) | async-done | bytes 1572880 | tf_op jit(solution)/shard_map/reduce_scatter | solution.py:252
  1506.2 202.7 %reduce-scatter.12.cloned.1.call-done = bf16[2,512,768]{2,1,0:T(8,128)(2,1)} async-done(((bf16[2,4096,768]{2,1,0:T(8,128)(2,1)}), bf16[2,512,768]{2,1,0:T(8,128)(2,1)}) %reduce-scatter.12.cloned.1.call-update) | async-done | bytes 1572880 | tf_op jit(solution)/shard_map/reduce_scatter | solution.py:255
  1725.4 10.2 bitcast_convert_fusion.2
  1737.1 9.7 bitcast_convert_fusion.1
  1748.2 9.9 bitcast_convert_fusion
  1761.6 26.4 %reduce-scatter.14.cloned.1.call-done = bf16[192,768]{1,0:T(8,128)(2,1)} async-done(((bf16[768,768]{1,0:T(8,128)(2,1)}), bf16[192,768]{1,0:T(8,128)(2,1)}) %reduce-scatter.14.cloned.1.call-update) | async-done | bytes 294928 | tf_op jit(solution)/shard_map/reduce_scatter | solution.py:275
  1788.1 50.4 %reduce-scatter.16.cloned.1.call-done = bf16[192,3072]{1,0:T(8,128)(2,1)} async-done(((bf16[768,3072]{1,0:T(8,128)(2,1)}), bf16[192,3072]{1,0:T(8,128)(2,1)}) %reduce-scatter.16.cloned.1.call-update) | async-done | bytes 1179664 | tf_op jit(solution)/shard_map/reduce_scatter | solution.py:278
  1838.5 50.5 %reduce-scatter.18.cloned.1.call-done = bf16[192,3072]{1,0:T(8,128)(2,1)} async-done(((bf16[768,3072]{1,0:T(8,128)(2,1)}), bf16[192,3072]{1,0:T(8,128)(2,1)}) %reduce-scatter.18.cloned.1.call-update) | async-done | bytes 1179664 | tf_op jit(solution)/shard_map/reduce_scatter | solution.py:281
  1889.0 50.4 %reduce-scatter.20.cloned.1.call-done = bf16[768,768]{1,0:T(8,128)(2,1)} async-done(((bf16[3072,768]{1,0:T(8,128)(2,1)}), bf16[768,768]{1,0:T(8,128)(2,1)}) %reduce-scatter.20.cloned.1.call-update) | async-done | bytes 1179664 | tf_op jit(solution)/shard_map/reduce_scatter | solution.py:284
  1942.2 10.1 all-reduce.10
  1952.7 22.7 %all-reduce.8 = (bf16[192]{0:T(256)(128)(2,1)S(1)}, bf16[192]{0:T(256)(128)(2,1)S(1)}, bf16[192]{0:T(256)(128)(2,1)S(1)}, bf16[192]{0:T(256)(128)(2,1)S(1)}) all-reduce(bf16[192]{0:T(256)(128)(2,1)S(1)} %dynamic-slice.5, bf16[192]{0:T(256)(128)(2,1)S(1)} %dynamic-slice.7, ...), channel_id=1, replica_groups=mesh['seq'=8,'shard'=4] {'seq'}, use_global_device_ids=true, to_apply=%region_28.29 | all-reduce | flops 768 | bytes 3072 | tf_op jit(solution)/shard_map/psum | solution.py:306
  1987.4 134.7 %all-reduce.14.cloned.1.call-done = (bf16[192,2304]{0,1:T(8,128)(2,1)}, bf16[192,768]{1,0:T(8,128)(2,1)}, bf16[192,3072]{1,0:T(8,128)(2,1)}, bf16[192,3072]{1,0:T(8,128)(2,1)}, bf16[768,768]{1,0:T(8,128)(2,1)}) async-done(((bf16[192,2304]{0,1:T(8,128)(2,1)}, bf16[192,768]{1,0:T(8,128)(2,1)}, bf16[192,3072]{1,0:T(8,128)(2,1)}, bf16[192,3072]{1,0:T(8,128)(2,1)}, bf16[768,768]{1,0:T(8,128)(2,1)}), ...) | async-done | bytes 4718608 | tf_op jit(solution)/shard_map/psum | solution.py:301
  (372 shorter events, 399.0 us)
Async XLA Ops:
  7.2 35.9 %all-gather.8.cloned.1.call-start = ((), (), s32[]{:S(2)}) async-start(), calls=%async_computation.7 | async-start | bytes 4423680 | tf_op jit(solution)/shard_map/all_gather | solution.py:157
  7.9 222.6 %all-gather.12.cloned.1.call-start = ((), (), s32[]{:S(2)}) async-start(), calls=%async_computation.9 | async-start | bytes 14155776 | tf_op jit(solution)/shard_map/all_gather | solution.py:183
  49.3 3.6 copy-start.16
  54.2 353.2 %all-gather.10.cloned.1.call-start = ((), (), s32[]{:S(2)}) async-start(), calls=%async_computation.8 | async-start | bytes 14155776 | tf_op jit(solution)/shard_map/all_gather | solution.py:182
  54.9 13.1 copy-start.27
  54.9 13.1 copy-start.29
  73.2 2.7 copy-start.46
  73.2 3.9 copy-start.47
  73.2 4.2 copy-start.48
  73.2 4.4 copy-start.49
  73.3 12.7 copy-start.17
  73.3 12.7 copy-start.18
  73.3 573.5 %all-gather.14.cloned.1.call-start = ((), (), s32[]{:S(2)}) async-start(), calls=%async_computation.10 | async-start | bytes 1474560 | tf_op jit(solution)/shard_map/all_gather | solution.py:158
  73.9 579.0 %all-gather.16.cloned.1.call-start = ((), (), s32[]{:S(2)}) async-start(), calls=%async_computation.11 | async-start | bytes 5898240 | tf_op jit(solution)/shard_map/all_gather | solution.py:159
  74.5 589.2 %all-gather.18.cloned.1.call-start = ((), (), s32[]{:S(2)}) async-start(), calls=%async_computation.12 | async-start | bytes 5898240 | tf_op jit(solution)/shard_map/all_gather | solution.py:160
  75.0 602.3 %all-gather.20.cloned.1.call-start = ((), (), s32[]{:S(2)}) async-start(), calls=%async_computation.13 | async-start | bytes 5898240 | tf_op jit(solution)/shard_map/all_gather | solution.py:161
  75.8 1422.9 %reduce-scatter.10.cloned.1.call-start = ((), (), s32[]{:S(2)}) async-start(), calls=%async_computation.14 | async-start | bytes 14155776 | tf_op jit(solution)/shard_map/reduce_scatter | solution.py:252
  409.8 2.3 copy-start.4
  438.4 2.3 copy-start.4
  468.0 2.3 copy-start.4
  497.8 2.4 copy-start.4
  528.5 2.3 copy-start.4
  557.9 2.3 copy-start.4
  587.3 2.3 copy-start.4
  616.7 2.3 copy-start.4
  643.8 6.9 copy-start.2
  646.7 4.0 copy-start.24
  652.8 10.8 copy-start.22
  686.6 35.4 %copy-start.5 = (f32[2,512,768]{2,1,0:T(8,128)}, f32[2,512,768]{2,1,0:T(8,128)S(1)}, u32[]{:S(2)}) copy-start(f32[2,512,768]{2,1,0:T(8,128)S(1)} %get-tuple-element.392) | copy-start | bytes 9437188
  686.6 2.5 copy-start.9
  686.6 2.5 copy-start.38
  686.6 35.4 %copy-start.36 = (f32[2,512]{1,0:T(2,128)}, f32[2,512]{1,0:T(2,128)S(1)}, u32[]{:S(2)}) copy-start(f32[2,512]{1,0:T(2,128)S(1)} %broadcast_multiply_fusion.5) | copy-start | bytes 12292
  689.1 32.8 %copy-start.40 = (f32[2,512]{1,0:T(2,128)}, f32[2,512]{1,0:T(2,128)S(1)}, u32[]{:S(2)}) copy-start(f32[2,512]{1,0:T(2,128)S(1)} %add_rsqrt_fusion) | copy-start | bytes 12292
  711.8 10.2 copy-start.8
  711.8 10.2 copy-start.10
  711.8 10.2 copy-start.51
  732.4 2.6 copy-start.31
  738.1 3.7 copy-start.1
  751.9 5.4 copy-start.3
  873.6 2.1 copy-start.26
  1141.0 2.1 copy-start.26
  1291.5 417.4 %reduce-scatter.12.cloned.1.call-start = ((), (), s32[]{:S(2)}) async-start(), calls=%async_computation.15 | async-start | bytes 14155776 | tf_op jit(solution)/shard_map/reduce_scatter | solution.py:255
  1292.2 467.1 %reduce-scatter.22.cloned.1.call-start = ((), (), s32[]{:S(2)}) async-start(), calls=%async_computation.20 | async-start | bytes 4423680
  1295.6 205.0 %copy-start.15 = (f32[2,512,12,64]{1,3,2,0:T(8,128)S(1)}, f32[2,512,12,64]{1,3,2,0:T(8,128)}, u32[]{:S(2)}) copy-start(f32[2,512,12,64]{1,3,2,0:T(8,128)} %broadcast_multiply_fusion) | copy-start | bytes 9437188
  1295.6 205.0 %copy-start.28 = (f32[2,512,32]{1,2,0:T(8,128)S(1)}, f32[2,512,32]{1,2,0:T(8,128)}, u32[]{:S(2)}) copy-start(f32[2,512,32]{1,2,0:T(8,128)} %copy-done.27) | copy-start | bytes 393220
  1295.6 205.0 %copy-start.30 = (f32[2,512,32]{1,2,0:T(8,128)S(1)}, f32[2,512,32]{1,2,0:T(8,128)}, u32[]{:S(2)}) copy-start(f32[2,512,32]{1,2,0:T(8,128)} %copy-done.29) | copy-start | bytes 393220
  1719.7 68.4 %reduce-scatter.14.cloned.1.call-start = ((), (), s32[]{:S(2)}) async-start(), calls=%async_computation.16 | async-start | bytes 1474560 | tf_op jit(solution)/shard_map/reduce_scatter | solution.py:275
  1725.4 113.1 %reduce-scatter.16.cloned.1.call-start = ((), (), s32[]{:S(2)}) async-start(), calls=%async_computation.17 | async-start | bytes 5898240 | tf_op jit(solution)/shard_map/reduce_scatter | solution.py:278
  1735.6 153.4 %reduce-scatter.18.cloned.1.call-start = ((), (), s32[]{:S(2)}) async-start(), calls=%async_computation.18 | async-start | bytes 5898240 | tf_op jit(solution)/shard_map/reduce_scatter | solution.py:281
  1746.8 192.6 %reduce-scatter.20.cloned.1.call-start = ((), (), s32[]{:S(2)}) async-start(), calls=%async_computation.19 | async-start | bytes 5898240 | tf_op jit(solution)/shard_map/reduce_scatter | solution.py:284
  1758.1 364.0 %all-reduce.14.cloned.1.call-start = ((), (), s32[]{:S(2)}) async-start(), calls=%async_computation.21 | async-start | bytes 10027008 | tf_op jit(solution)/shard_map/psum | solution.py:301
  1939.4 2.8 copy-start.42
  1939.4 2.8 copy-start.44
  1939.4 2.8 copy-start.45
  1939.4 38.2 %copy-start.6 = (f32[2,512,768]{2,1,0:T(8,128)S(1)}, f32[2,512,768]{2,1,0:T(8,128)}, u32[]{:S(2)}) copy-start(f32[2,512,768]{2,1,0:T(8,128)} %copy-done.5) | copy-start | bytes 9437188
  1939.4 38.2 %copy-start.37 = (f32[2,512]{1,0:T(2,128)S(1)}, f32[2,512]{1,0:T(2,128)}, u32[]{:S(2)}) copy-start(f32[2,512]{1,0:T(2,128)} %copy-done.36) | copy-start | bytes 12292
  1939.4 38.2 %copy-start.39 = (f32[768]{0:T(1024)S(1)}, f32[768]{0:T(1024)}, u32[]{:S(2)}) copy-start(f32[768]{0:T(1024)} %convert_element_type.173) | copy-start | bytes 9220
  1939.4 38.2 %copy-start.41 = (f32[2,512]{1,0:T(2,128)S(1)}, f32[2,512]{1,0:T(2,128)}, u32[]{:S(2)}) copy-start(f32[2,512]{1,0:T(2,128)} %copy-done.40) | copy-start | bytes 12292
  1975.3 4.0 copy-start.14
  1975.3 4.0 copy-start.21
  2122.1 2.6 copy-start.35
  2122.1 3.5 copy-start.34
  2122.1 5.2 copy-start.33
  2125.6 3.3 copy-start.32
  (24 other events, 40.4 us)
Sparse Core Ops, SparseCore 0:
  9.5 33.4 all-gather.7
  54.4 176.0 all-gather.11
  233.1 174.2 all-gather.9
  408.9 15.6 all-gather.13
  425.9 37.4 all-gather.15
  464.8 37.4 all-gather.17
  503.8 37.4 all-gather.19
  1291.6 207.1 reduce-scatter.9
  1502.3 206.5 reduce-scatter.11
  1719.8 39.4 reduce-scatter.21
  1762.4 25.5 reduce-scatter.13
  1790.5 47.9 reduce-scatter.15
  1841.0 47.9 reduce-scatter.17
  1891.4 47.9 reduce-scatter.19
  1944.1 178.0 all-reduce.13
where the time goes:
time: 2150 us; the launch traced here: 2140 us
  waiting for transfers between devices  1060 us (49%)
  matrix products  775 us (36%)
  local copies, waits for them, and re-layouts  181 us (8%)
  other arithmetic  50.1 us (2%)
  blocking collectives  39.5 us (2%)
    reduce_scatter x1, waiting for transfers between devices, local(): lax.psum_scatter(k_all.astype(jnp.bfloat16), 'seq', scatter_dimension=1,...  203 us
    reduce_scatter x1, waiting for transfers between devices, local(): lax.psum_scatter(v_all.astype(jnp.bfloat16), 'seq', scatter_dimension=1,...  203 us
    all_gather x1, waiting for transfers between devices, local(): lax.all_gather(k_local, 'seq', axis=1, tiled=True)  161 us
    all_gather x1, waiting for transfers between devices, local(): lax.all_gather(v_local, 'seq', axis=1, tiled=True)  144 us
    psum x1, waiting for transfers between devices, local(): lax.psum(owned[0].astype(jnp.bfloat16), 'seq').astype(jnp.float32)  135 us
    dot_general x8, matrix products, back_step(): jnp.einsum('sqhd,skhd->shqk', g_heads, v_part, preferred_element_type=jnp...  127 us
    dot_general x8, matrix products, attend_step(): jnp.einsum('shqk,skhd->sqhd', expo.astype(jnp.bfloat16), v_part, preferre...  107 us
    dot_general x8, matrix products, back_step(): jnp.einsum('shqk,sqhd->skhd', expo.astype(jnp.bfloat16), g_heads, preferr...  93.2 us
  transfers between devices with their start and end apart: 15, of which 11 were waited for; matrix products, arithmetic and copies ran while one was open for 17% of the time, Pallas kernels for 0%

commit v1 on v0

--- a/solution.py
+++ b/solution.py
@@ -8,6 +8,11 @@
 HD = 64
 EPS = 1e-05
 ROPE_BASE = 1000.0
+
+
+def exchange_gather(block, axis, dim):
+    sent = jnp.stack([block] * lax.axis_size(axis))
+    return jnp.concatenate(lax.all_to_all(sent, axis, 0, 0), axis=dim)
 
 
 def rope_tables(pos_block):
@@ -179,7 +184,7 @@
     k_local = k_heads.reshape(seq_count, row_count, model_width)
     v_local = v_heads.reshape(seq_count, row_count, model_width)
     k_full, v_full = (
-        lax.all_gather(k_local, "seq", axis=1, tiled=True),
+        exchange_gather(k_local, "seq", 1),
         lax.all_gather(v_local, "seq", axis=1, tiled=True),
     )
     row_total, value_sum = attend(q_heads, q_seg, k_full, v_full, segments, row_count, score_scale)

time: 2150 us -> 2280 us (1.060)
  waiting for transfers between devices: 1060 us -> 1150 us
  local copies, waits for them, and re-layouts: 181 us -> 227 us
    all_to_all x0 -> x1, waiting for transfers between devices: none -> 393 us  [exchange_gather(): return jnp.concatenate(lax.all_to_all(sent, axis, 0, 0), axis=dim)]
    all_gather x1, waiting for transfers between devices: 161 us -> 0.02 us  [local(): lax.all_gather(k_local, 'seq', axis=1, tiled=True)]
    all_gather x1, waiting for transfers between devices: 144 us -> 0.01 us  [local(): lax.all_gather(v_local, 'seq', axis=1, tiled=True)]
    dynamic_slice x0 -> x16, local copies, waits for them, and re-layouts: none -> 26.5 us  [attend_step(): lax.dynamic_slice_in_dim(k_full, start, block, 1)]
    dot_general x8, matrix products: 107 us -> 84.4 us  [attend_step(): jnp.einsum('shqk,skhd->sqhd', expo.astype(jnp.bfloat16), v_part, preferre...]
  transfers between devices with their start and end apart: 15 -> 16, of which waited for: 11 -> 10; matrix products, arithmetic and copies ran while one was open for 17% -> 20% of each run, Pallas kernels for 0% -> 0%
where the time goes in v1:
time: 2280 us; the launch traced here: 2270 us
  waiting for transfers between devices  1150 us (50%)
  matrix products  773 us (34%)
  local copies, waits for them, and re-layouts  227 us (10%)
  other arithmetic  49.6 us (2%)
  blocking collectives  38.9 us (2%)
    all_to_all x1, waiting for transfers between devices, exchange_gather(): return jnp.concatenate(lax.all_to_all(sent, axis, 0, 0), axis=dim)  393 us
    reduce_scatter x1, waiting for transfers between devices, local(): lax.psum_scatter(k_all.astype(jnp.bfloat16), 'seq', scatter_dimension=1,...  203 us
    reduce_scatter x1, waiting for transfers between devices, local(): lax.psum_scatter(v_all.astype(jnp.bfloat16), 'seq', scatter_dimension=1,...  203 us
    psum x1, waiting for transfers between devices, local(): lax.psum(owned[0].astype(jnp.bfloat16), 'seq').astype(jnp.float32)  135 us
    dot_general x8, matrix products, back_step(): jnp.einsum('sqhd,skhd->shqk', g_heads, v_part, preferred_element_type=jnp...  126 us
    dot_general x8, matrix products, attend_step(): jnp.einsum('sqhd,skhd->shqk', q_heads, k_part, preferred_element_type=jnp...  108 us
    dot_general x8, matrix products, back_step(): jnp.einsum('sqhd,skhd->shqk', q_heads, k_part, preferred_element_type=jnp...  92.3 us
    dot_general x8, matrix products, attend_step(): jnp.einsum('shqk,skhd->sqhd', expo.astype(jnp.bfloat16), v_part, preferre...  84.4 us
  transfers between devices with their start and end apart: 16, of which 10 were waited for; matrix products, arithmetic and copies ran while one was open for 20% of the time, Pallas kernels for 0%

profile of v1, /device:TPU:0, one launch (start us, length us, event | category | flops | bytes accessed | tf_op | source)
XLA Modules:
  0.0 2273.6 jit_solution(6400160967736142496)
XLA Ops:
  8.0 35.1 %all-gather.8.cloned.1.call-done = bf16[768,2304]{1,0:T(8,128)(2,1)} async-done(((bf16[192,2304]{1,0:T(8,128)(2,1)}), bf16[768,2304]{1,0:T(8,128)(2,1)}) %all-gather.8.cloned.1.call-update) | async-done | bytes 3538960 | tf_op jit(solution)/shard_map/all_gather | solution.py:162
  97.2 392.7 %all-to-all-done = bf16[8,2,512,768]{2,3,1,0:T(8,128)(2,1)} async-done(((bf16[8,2,512,768]{2,3,1,0:T(8,128)(2,1)}), bf16[8,2,512,768]{2,3,1,0:T(8,128)(2,1)}, u32[]{:S(2)}, u32[]{:S(2)}) %all-to-all-start) | async-done | bytes 12582944 | tf_op jit(solution)/shard_map/all_to_all | solution.py:15
  489.9 16.7 copy.86
  506.7 16.0 copy.89
  522.7 271.7 %while.28 = (s32[]{:T(128)}, f32[2,12,512]{2,1,0:T(8,128)S(1)}, f32[2,512,12,64]{1,3,2,0:T(8,128)}, s32[2,512]{1,0:T(2,128)S(1)}, s32[8]{0:T(128)S(1)}, /*index=...) while((s32[]{:T(128)}, f32[2,12,512]{2,1,0:T(8,128)S(1)}, ...), condition=%wide.region_2.3_spmd.clone, body=%wide.region_0.2_spmd.clone.sunk | while | flops 1650470912 | bytes 99828008 | solution.py:91
  528.5 13.7 fusion.117
  544.5 10.6 bitcast_add_fusion.4
  562.6 13.3 fusion.117
  578.3 10.6 bitcast_add_fusion.4
  596.3 14.2 fusion.117
  613.1 10.5 bitcast_add_fusion.4
  631.0 13.3 fusion.117
  646.7 10.6 bitcast_add_fusion.4
  664.8 13.8 fusion.117
  681.0 10.7 bitcast_add_fusion.4
  699.1 13.3 fusion.117
  714.9 10.5 bitcast_add_fusion.4
  732.8 13.4 fusion.117
  748.6 10.5 bitcast_add_fusion.4
  766.6 13.1 fusion.117
  782.1 10.5 bitcast_add_fusion.4
  802.5 10.8 fusion.31
  813.3 13.7 multiply_convert_fusion.2
  827.0 9.2 fusion.65
  842.7 18.8 multiply_convert_fusion.1
  861.6 10.2 fusion.25
  871.8 10.5 multiply_reduce_fusion
  907.1 521.5 %while.29 = (s32[]{:T(128)}, f32[2,512,12,64]{1,3,2,0:T(8,128)}, bf16[2,4096,768]{1,2,0:T(8,128)(2,1)}, bf16[2,4096,768]{2,1,0:T(8,128)(2,1)}, s32[8]{0:T(128)S(...) while((s32[]{:T(128)}, f32[2,512,12,64]{1,3,2,0:T(8,128)}, ...), condition=%wide.region_13.14_spmd.clone, body=%wide.region_12.13_spmd.clone.sunk | while | flops 4080533504 | bytes 159449392 | solution.py:139
  910.8 11.5 fusion.128
  924.2 15.8 fusion.129
  959.3 10.5 fusion.130
  975.2 11.5 fusion.128
  988.5 15.8 fusion.129
  1024.5 10.5 fusion.130
  1040.4 11.5 fusion.128
  1053.8 15.8 fusion.129
  1089.8 10.5 fusion.130
  1105.7 11.5 fusion.128
  1119.0 15.8 fusion.129
  1155.0 10.5 fusion.130
  1171.0 11.5 fusion.128
  1184.4 15.8 fusion.129
  1220.4 10.5 fusion.130
  1236.2 11.5 fusion.128
  1249.6 15.8 fusion.129
  1285.6 10.5 fusion.130
  1301.5 11.5 fusion.128
  1314.9 15.8 fusion.129
  1350.9 10.5 fusion.130
  1366.7 11.5 fusion.128
  1380.1 15.8 fusion.129
  1416.1 10.5 fusion.130
  1432.8 202.9 %reduce-scatter.10.cloned.1.call-done = bf16[2,512,768]{1,2,0:T(8,128)(2,1)} async-done(((bf16[2,4096,768]{1,2,0:T(8,128)(2,1)}), bf16[2,512,768]{1,2,0:T(8,128)(2,1)}) %reduce-scatter.10.cloned.1.call-update) | async-done | bytes 1572880 | tf_op jit(solution)/shard_map/reduce_scatter | solution.py:257
  1643.1 202.7 %reduce-scatter.12.cloned.1.call-done = bf16[2,512,768]{2,1,0:T(8,128)(2,1)} async-done(((bf16[2,4096,768]{2,1,0:T(8,128)(2,1)}), bf16[2,512,768]{2,1,0:T(8,128)(2,1)}) %reduce-scatter.12.cloned.1.call-update) | async-done | bytes 1572880 | tf_op jit(solution)/shard_map/reduce_scatter | solution.py:260
  1862.4 10.2 bitcast_convert_fusion.2
  1874.1 9.7 bitcast_convert_fusion.1
  1885.1 9.9 bitcast_convert_fusion
  1898.6 25.9 %reduce-scatter.14.cloned.1.call-done = bf16[192,768]{1,0:T(8,128)(2,1)} async-done(((bf16[768,768]{1,0:T(8,128)(2,1)}), bf16[192,768]{1,0:T(8,128)(2,1)}) %reduce-scatter.14.cloned.1.call-update) | async-done | bytes 294928 | tf_op jit(solution)/shard_map/reduce_scatter | solution.py:280
  1924.5 50.4 %reduce-scatter.16.cloned.1.call-done = bf16[192,3072]{1,0:T(8,128)(2,1)} async-done(((bf16[768,3072]{1,0:T(8,128)(2,1)}), bf16[192,3072]{1,0:T(8,128)(2,1)}) %reduce-scatter.16.cloned.1.call-update) | async-done | bytes 1179664 | tf_op jit(solution)/shard_map/reduce_scatter | solution.py:283
  1974.8 50.5 %reduce-scatter.18.cloned.1.call-done = bf16[192,3072]{1,0:T(8,128)(2,1)} async-done(((bf16[768,3072]{1,0:T(8,128)(2,1)}), bf16[192,3072]{1,0:T(8,128)(2,1)}) %reduce-scatter.18.cloned.1.call-update) | async-done | bytes 1179664 | tf_op jit(solution)/shard_map/reduce_scatter | solution.py:286
  2025.3 50.4 %reduce-scatter.20.cloned.1.call-done = bf16[768,768]{1,0:T(8,128)(2,1)} async-done(((bf16[3072,768]{1,0:T(8,128)(2,1)}), bf16[768,768]{1,0:T(8,128)(2,1)}) %reduce-scatter.20.cloned.1.call-update) | async-done | bytes 1179664 | tf_op jit(solution)/shard_map/reduce_scatter | solution.py:289
  2078.6 10.1 all-reduce.10
  2089.0 22.7 all-reduce.8
  2123.7 134.8 %all-reduce.14.cloned.1.call-done = (bf16[192,2304]{0,1:T(8,128)(2,1)}, bf16[192,768]{1,0:T(8,128)(2,1)}, bf16[192,3072]{1,0:T(8,128)(2,1)}, bf16[192,3072]{1,0:T(8,128)(2,1)}, bf16[768,768]{1,0:T(8,128)(2,1)}) async-done(((bf16[192,2304]{0,1:T(8,128)(2,1)}, bf16[192,768]{1,0:T(8,128)(2,1)}, bf16[192,3072]{1,0:T(8,128)(2,1)}, bf16[192,3072]{1,0:T(8,128)(2,1)}, bf16[768,768]{1,0:T(8,128)(2,1)}), ...) | async-done | bytes 4718608 | tf_op jit(solution)/shard_map/psum | solution.py:306
  (424 shorter events, 436.7 us)
Async XLA Ops:
  7.2 35.9 %all-gather.8.cloned.1.call-start = ((), (), s32[]{:S(2)}) async-start(), calls=%async_computation.8 | async-start | bytes 4423680 | tf_op jit(solution)/shard_map/all_gather | solution.py:162
  7.9 498.8 %all-gather.10.cloned.1.call-start = ((), (), s32[]{:S(2)}) async-start(), calls=%async_computation.9 | async-start | bytes 14155776 | tf_op jit(solution)/shard_map/all_gather | solution.py:188
  49.3 3.6 copy-start.17
  54.2 742.7 %all-gather.12.cloned.1.call-start = ((), (), s32[]{:S(2)}) async-start(), calls=%async_computation.10 | async-start | bytes 1474560 | tf_op jit(solution)/shard_map/all_gather | solution.py:163
  55.6 13.0 copy-start.28
  55.6 13.0 copy-start.30
  72.7 5.7 copy-start.9
  78.4 411.5 %all-to-all-start = ((bf16[8,2,512,768]{2,3,1,0:T(8,128)(2,1)}), bf16[8,2,512,768]{2,3,1,0:T(8,128)(2,1)}, u32[]{:S(2)}, u32[]{:S(2)}) async-start(bf16[8,2,512,768]{2,3,1,0:T(8,128)(2,1)} %stack.3), calls=%async_computation | async-start | bytes 25165824 | tf_op jit(solution)/shard_map/all_to_all | solution.py:15
  84.1 3.2 copy-start.49
  84.1 3.4 copy-start.50
  84.1 3.6 copy-start.51
  84.1 11.8 copy-start.18
  84.1 11.8 copy-start.19
  84.1 718.4 %all-gather.14.cloned.1.call-start = ((), (), s32[]{:S(2)}) async-start(), calls=%async_computation.11 | async-start | bytes 5898240 | tf_op jit(solution)/shard_map/all_gather | solution.py:164
  84.7 728.6 %all-gather.16.cloned.1.call-start = ((), (), s32[]{:S(2)}) async-start(), calls=%async_computation.12 | async-start | bytes 5898240 | tf_op jit(solution)/shard_map/all_gather | solution.py:165
  85.3 741.7 %all-gather.18.cloned.1.call-start = ((), (), s32[]{:S(2)}) async-start(), calls=%async_computation.13 | async-start | bytes 5898240 | tf_op jit(solution)/shard_map/all_gather | solution.py:166
  85.9 809.7 %all-gather.20.cloned.1.call-start = ((), (), s32[]{:S(2)}) async-start(), calls=%async_computation.14 | async-start | bytes 14155776 | tf_op jit(solution)/shard_map/all_gather | solution.py:223
  95.4 1540.3 %reduce-scatter.10.cloned.1.call-start = ((), (), s32[]{:S(2)}) async-start(), calls=%async_computation.15 | async-start | bytes 14155776 | tf_op jit(solution)/shard_map/reduce_scatter | solution.py:257
  525.0 3.4 copy-start.4
  559.3 3.3 copy-start.4
  593.0 3.3 copy-start.4
  610.5 2.6 copy-start.1
  627.7 3.3 copy-start.4
  661.5 3.3 copy-start.4
  678.5 2.5 copy-start.1
  695.8 3.3 copy-start.4
  729.5 3.3 copy-start.4
  763.3 3.3 copy-start.4
  794.4 2.5 copy-start.48
  796.9 3.5 copy-start.25
  802.5 10.8 copy-start.23
  836.3 35.5 %copy-start.5 = (f32[2,512,768]{2,1,0:T(8,128)}, f32[2,512,768]{2,1,0:T(8,128)S(1)}, u32[]{:S(2)}) copy-start(f32[2,512,768]{2,1,0:T(8,128)S(1)} %get-tuple-element.422) | copy-start | bytes 9437188
  836.3 2.5 copy-start.10
  836.3 2.5 copy-start.39
  836.3 35.4 %copy-start.37 = (f32[2,512]{1,0:T(2,128)}, f32[2,512]{1,0:T(2,128)S(1)}, u32[]{:S(2)}) copy-start(f32[2,512]{1,0:T(2,128)S(1)} %broadcast_multiply_fusion.5) | copy-start | bytes 12292
  838.8 32.9 %copy-start.41 = (f32[2,512]{1,0:T(2,128)}, f32[2,512]{1,0:T(2,128)S(1)}, u32[]{:S(2)}) copy-start(f32[2,512]{1,0:T(2,128)S(1)} %add_rsqrt_fusion) | copy-start | bytes 12292
  861.6 10.2 copy-start.8
  861.6 10.2 copy-start.11
  861.6 10.2 copy-start.53
  882.3 2.6 copy-start.32
  888.0 3.7 copy-start.3
  1428.7 417.2 %reduce-scatter.12.cloned.1.call-start = ((), (), s32[]{:S(2)}) async-start(), calls=%async_computation.16 | async-start | bytes 14155776 | tf_op jit(solution)/shard_map/reduce_scatter | solution.py:260
  1429.4 466.8 %reduce-scatter.22.cloned.1.call-start = ((), (), s32[]{:S(2)}) async-start(), calls=%async_computation.21 | async-start | bytes 4423680
  1432.8 204.8 %copy-start.16 = (f32[2,512,12,64]{1,3,2,0:T(8,128)S(1)}, f32[2,512,12,64]{1,3,2,0:T(8,128)}, u32[]{:S(2)}) copy-start(f32[2,512,12,64]{1,3,2,0:T(8,128)} %broadcast_multiply_fusion) | copy-start | bytes 9437188
  1432.8 204.8 %copy-start.29 = (f32[2,512,32]{1,2,0:T(8,128)S(1)}, f32[2,512,32]{1,2,0:T(8,128)}, u32[]{:S(2)}) copy-start(f32[2,512,32]{1,2,0:T(8,128)} %copy-done.28) | copy-start | bytes 393220
  1432.8 204.8 %copy-start.31 = (f32[2,512,32]{1,2,0:T(8,128)S(1)}, f32[2,512,32]{1,2,0:T(8,128)}, u32[]{:S(2)}) copy-start(f32[2,512,32]{1,2,0:T(8,128)} %copy-done.30) | copy-start | bytes 393220
  1856.6 67.9 %reduce-scatter.14.cloned.1.call-start = ((), (), s32[]{:S(2)}) async-start(), calls=%async_computation.17 | async-start | bytes 1474560 | tf_op jit(solution)/shard_map/reduce_scatter | solution.py:280
  1862.3 112.5 %reduce-scatter.16.cloned.1.call-start = ((), (), s32[]{:S(2)}) async-start(), calls=%async_computation.18 | async-start | bytes 5898240 | tf_op jit(solution)/shard_map/reduce_scatter | solution.py:283
  1872.6 152.8 %reduce-scatter.18.cloned.1.call-start = ((), (), s32[]{:S(2)}) async-start(), calls=%async_computation.19 | async-start | bytes 5898240 | tf_op jit(solution)/shard_map/reduce_scatter | solution.py:286
  1883.7 192.0 %reduce-scatter.20.cloned.1.call-start = ((), (), s32[]{:S(2)}) async-start(), calls=%async_computation.20 | async-start | bytes 5898240 | tf_op jit(solution)/shard_map/reduce_scatter | solution.py:289
  1895.1 363.4 %all-reduce.14.cloned.1.call-start = ((), (), s32[]{:S(2)}) async-start(), calls=%async_computation.22 | async-start | bytes 10027008 | tf_op jit(solution)/shard_map/psum | solution.py:306
  2075.7 2.8 copy-start.43
  2075.7 2.8 copy-start.45
  2075.7 2.8 copy-start.46
  2075.7 38.2 %copy-start.6 = (f32[2,512,768]{2,1,0:T(8,128)S(1)}, f32[2,512,768]{2,1,0:T(8,128)}, u32[]{:S(2)}) copy-start(f32[2,512,768]{2,1,0:T(8,128)} %copy-done.5) | copy-start | bytes 9437188
  2075.7 38.2 %copy-start.38 = (f32[2,512]{1,0:T(2,128)S(1)}, f32[2,512]{1,0:T(2,128)}, u32[]{:S(2)}) copy-start(f32[2,512]{1,0:T(2,128)} %copy-done.37) | copy-start | bytes 12292
  2075.7 38.2 %copy-start.40 = (f32[768]{0:T(1024)S(1)}, f32[768]{0:T(1024)}, u32[]{:S(2)}) copy-start(f32[768]{0:T(1024)} %convert_element_type.175) | copy-start | bytes 9220
  2075.7 38.2 %copy-start.42 = (f32[2,512]{1,0:T(2,128)S(1)}, f32[2,512]{1,0:T(2,128)}, u32[]{:S(2)}) copy-start(f32[2,512]{1,0:T(2,128)} %copy-done.41) | copy-start | bytes 12292
  2111.7 4.0 copy-start.15
  2111.7 4.0 copy-start.22
  2258.4 2.6 copy-start.36
  2258.4 3.5 copy-start.35
  2258.4 5.2 copy-start.34
  2261.9 3.3 copy-start.33
  (41 other events, 76.3 us)
Sparse Core Ops, SparseCore 0:
  9.5 33.4 all-gather.7
  54.4 408.8 all-gather.9
  464.9 14.6 all-gather.11
  481.0 37.4 all-gather.13
  519.9 37.4 all-gather.15
  558.7 37.4 all-gather.17
  598.8 176.1 all-gather.19
  1428.8 206.8 reduce-scatter.9
  1639.3 206.5 reduce-scatter.11
  1856.7 39.4 reduce-scatter.21
  1898.8 25.6 reduce-scatter.13
  1926.9 47.9 reduce-scatter.15
  1977.4 47.9 reduce-scatter.17
  2027.7 47.9 reduce-scatter.19
  2080.4 178.0 all-reduce.13
